TPU v7x, 512 devices: a whole 4x8x8 slice. The times are simulated.
512 devices in a mesh: seq: 128 (over z, y, core), head: 4 (over x).
Axes of the slice: x: 4, y: 8, z: 8, core: 2. Of those that a mesh axis runs over, the one named last changes fastest.
Arguments:
- hidden_states: bfloat16 [32768, 2048], P('seq', 'head'), may hold values from -0.375 to 0.375
- w_lambda: bfloat16 [2048, 512], P('head'), may hold values from -2 to 2
- queries: bfloat16 [32768, 2048], P('seq', 'head'), may hold values from -6 to 6
- keys: bfloat16 [32768, 2048], P('seq', 'head'), may hold values from -0.01171875 to 0.01171875
- values: bfloat16 [32768, 4096], P('seq', 'head'), may hold values from -6 to 6
- d_out: bfloat16 [32768, 4096], P('seq', 'head'), may hold values from -0.75 to 0.75
- d_state: float32 [32, 64, 128], P('head'), may hold values from -6 to 6
Outputs:
- out: bfloat16 [32768, 4096], P('seq', 'head')
- d_queries: bfloat16 [32768, 2048], P('seq', 'head')
- d_keys: bfloat16 [32768, 2048], P('seq', 'head')
- d_values: bfloat16 [32768, 4096], P('seq', 'head')
- d_hidden: bfloat16 [32768, 2048], P('seq', 'head')
- d_w_lambda: float32 [2048, 512], P(('head', 'seq'))
All inputs are finite; a program needn't handle non-finite values.
Results may differ from a plain program's by a relative error of at most 0.0049.
Values may be sent and summed in bfloat16 or wider, within the bound.
A program may use at most 64 MiB of HBM per device.

v0:
```python
import jax
import jax.numpy as jnp
from jax import lax
from jax.sharding import Mesh
from jax.sharding import PartitionSpec as P

H = 32
DK = 64
DV = 128
SEQ = ("seq_0", "seq_1", "seq_2")
HEAD_SEQ = ("head", "seq_0", "seq_1", "seq_2")


PRECISE = lax.Precision.HIGHEST


def cut_along(shard, dim, length):
    before, after = (shard.shape[:dim], shard.shape[dim + 1 :])
    return jnp.moveaxis(shard.reshape(*before, length, -1, *after), dim, 0)


def summed_on_arrival(shard, axis, dim):
    pieces = cut_along(shard, dim, lax.axis_size(axis))
    arrived = lax.all_to_all(pieces, axis, split_axis=0, concat_axis=0, tiled=True)
    return arrived.sum(axis=0)


def partner_2(value, axis, stride):
    mask = 2**stride
    pairs = [(source, source ^ mask) for source in range(lax.axis_size(axis))]
    return lax.ppermute(value, axis, pairs)


def copy_for_each(shard, axis):
    copies = jnp.broadcast_to(shard, (lax.axis_size(axis), *shard.shape))
    return lax.all_to_all(copies, axis, split_axis=0, concat_axis=0, tiled=True)


def laid_out(pieces, dim):
    pieces = jnp.moveaxis(pieces, 0, dim)
    lengths = pieces.shape
    return pieces.reshape(*lengths[:dim], lengths[dim] * lengths[dim + 1], *lengths[dim + 2 :])


def collect(shard, axis, dim):
    pieces = copy_for_each(shard, axis)
    return laid_out(pieces, dim)


def sum_by_axis(shard, axes, dim):
    far, near = axes
    pieces = cut_along(shard, dim, lax.axis_size(far))
    nearer = summed_on_arrival(pieces, near, dim + 1)
    arrived = lax.all_to_all(nearer, far, split_axis=0, concat_axis=0, tiled=True)
    return arrived.sum(axis=0)


def digit_count(values, width):
    total = jnp.zeros_like(values)
    for shift in range(width):
        total = total + (values >> shift > 0).astype(jnp.int32)
    return total


def level_table(row_count, width, levels):
    later = jnp.arange(row_count, dtype=jnp.int32)[:, None]
    earlier = jnp.arange(row_count, dtype=jnp.int32)[None, :]
    depth = digit_count(jnp.bitwise_xor(later, earlier), width)
    keep = earlier <= later
    grid = jnp.arange(levels, dtype=jnp.int32)[:, None, None]
    return jnp.where((depth[None] == grid) & keep[None], 1.0, 0.0).astype(jnp.float32)


def pick_table(width, seq_bits, levels):
    wanted = width + 1 + jnp.arange(seq_bits, dtype=jnp.int32)
    return jnp.where(
        jnp.arange(levels, dtype=jnp.int32)[None, :] == wanted[:, None], 1.0, 0.0
    ).astype(jnp.float32)


def local_pass(
    query_heads, key_heads, value_heads, level_weights, table, states, picks, grad_heads
):
    query_wide = query_heads.astype(jnp.float32)
    grad_wide = grad_heads.astype(jnp.float32)
    scores = jnp.einsum("thd,shd->hts", query_heads, key_heads, preferred_element_type=jnp.float32)
    spread = jnp.einsum("thl,lts->hts", level_weights, table, precision=PRECISE)
    mixed = (scores * spread).astype(jnp.bfloat16)
    local_out = jnp.einsum("hts,shv->thv", mixed, value_heads, preferred_element_type=jnp.float32)
    chosen = jnp.einsum("thl,kl->thk", level_weights, picks, precision=PRECISE)
    scaled = chosen[:, :, :, None] * query_wide[:, :, None, :]
    carried = jnp.einsum("thkd,khdv->thv", scaled, states, precision=PRECISE)
    result = (local_out + carried).astype(jnp.bfloat16)
    grad_mixed = jnp.einsum(
        "thv,shv->hts", grad_heads, value_heads, preferred_element_type=jnp.float32
    )
    grad_values = jnp.einsum("hts,thv->shv", mixed, grad_heads, preferred_element_type=jnp.float32)
    grad_scores = (grad_mixed * spread).astype(jnp.bfloat16)
    grad_weights = jnp.einsum("hts,lts->thl", grad_mixed * scores, table, precision=PRECISE)
    grad_queries = jnp.einsum(
        "hts,shd->thd", grad_scores, key_heads, preferred_element_type=jnp.float32
    )
    grad_keys = jnp.einsum(
        "hts,thd->shd", grad_scores, query_heads, preferred_element_type=jnp.float32
    )
    grad_scaled = jnp.einsum("thv,khdv->thkd", grad_wide, states, precision=PRECISE)
    grad_queries = grad_queries + jnp.einsum(
        "thk,thkd->thd", chosen, grad_scaled, precision=PRECISE
    )
    grad_chosen = jnp.einsum("thkd,thd->thk", grad_scaled, query_wide, precision=PRECISE)
    grad_weights = grad_weights + jnp.einsum("thk,kl->thl", grad_chosen, picks, precision=PRECISE)
    grad_states = jnp.einsum("thkd,thv->khdv", scaled, grad_wide, precision=PRECISE)
    return (result, grad_queries, grad_keys, grad_values, grad_weights, grad_states)


def body(hidden_states, w_lambda, queries, keys, values, d_out, d_state):
    row_count = hidden_states.shape[0]
    heads = queries.shape[1] // DK
    levels = w_lambda.shape[1] // H
    tok_bits = row_count.bit_length() - 1
    seq_bits = lax.axis_size(SEQ).bit_length() - 1
    index = lax.axis_index(SEQ)
    partial_terms = jnp.dot(hidden_states, w_lambda, preferred_element_type=jnp.float32)
    projected = summed_on_arrival(partial_terms, "head", 1)
    level_weights = jax.nn.softplus(projected).reshape(row_count, heads, levels)
    query_heads = queries.reshape(row_count, heads, DK)
    key_heads = keys.reshape(row_count, heads, DK)
    value_heads = values.reshape(row_count, heads, DV)
    grad_heads = d_out.reshape(row_count, heads, DV)
    kv_state = jnp.einsum(
        "thd,thv->hdv", key_heads, value_heads, preferred_element_type=jnp.float32
    )
    top_count = 0
    low_count = seq_bits - top_count
    uppers = []
    total = kv_state
    for bit in range(low_count):
        partner = partner_2(total, SEQ, bit)
        is_upper = index >> bit & 1 == 1
        uppers.append(jnp.where(is_upper, partner, 0.0))
        total = total + partner
    states = jnp.stack(uppers, 0)
    table = level_table(row_count, tok_bits, levels)
    picks = pick_table(tok_bits, seq_bits, levels)
    result, grad_queries, grad_keys, grad_values, grad_weights, state_grads = local_pass(
        query_heads, key_heads, value_heads, level_weights, table, states, picks, grad_heads
    )
    leader = index % (1 << low_count) == 0
    adjoint = jnp.where(leader, d_state, 0.0)
    for bit in reversed(range(low_count)):
        is_upper = index >> bit & 1 == 1
        pending = adjoint + jnp.where(is_upper, state_grads[bit], 0.0)
        adjoint = adjoint + partner_2(pending, SEQ, bit)
    grad_keys = grad_keys + jnp.einsum(
        "thv,hdv->thd", value_heads.astype(jnp.float32), adjoint, precision=PRECISE
    )
    grad_values = grad_values + jnp.einsum(
        "thd,hdv->thv", key_heads.astype(jnp.float32), adjoint, precision=PRECISE
    )
    grad_projected = (
        grad_weights.reshape(row_count, heads * levels) * jax.nn.sigmoid(projected)
    ).astype(jnp.bfloat16)
    gathered = collect(grad_projected, "head", 1)
    d_hidden = jnp.einsum(
        "tc,dc->td", gathered, w_lambda, preferred_element_type=jnp.float32
    ).astype(jnp.bfloat16)
    d_w_lambda = sum_by_axis(
        jnp.einsum("td,tc->dc", hidden_states, gathered, preferred_element_type=jnp.float32),
        (("seq_0", "seq_1"), "seq_2"),
        0,
    )
    out = result.reshape(row_count, heads * DV)
    d_queries = grad_queries.reshape(row_count, heads * DK).astype(jnp.bfloat16)
    d_keys = grad_keys.reshape(row_count, heads * DK).astype(jnp.bfloat16)
    d_values = grad_values.reshape(row_count, heads * DV).astype(jnp.bfloat16)
    return (out, d_queries, d_keys, d_values, d_hidden, d_w_lambda)


def solution(mesh):
    split = Mesh(
        mesh.devices.reshape(8, 8, 2, mesh.shape["head"]), ("seq_0", "seq_1", "seq_2", "head")
    )
    in_specs = (
        P(SEQ, "head"),
        P("head", None),
        P(SEQ, "head"),
        P(SEQ, "head"),
        P(SEQ, "head"),
        P(SEQ, "head"),
        P("head", None, None),
    )
    out_specs = (
        P(SEQ, "head"),
        P(SEQ, "head"),
        P(SEQ, "head"),
        P(SEQ, "head"),
        P(SEQ, "head"),
        P(HEAD_SEQ, None),
    )
    return jax.shard_map(body, mesh=split, in_specs=in_specs, out_specs=out_specs, check_vma=False)
```

profile of v0, /device:TPU:1, one launch (start us, length us, event | category | flops | bytes accessed | tf_op | source)
XLA Modules:
  0.0 232.9 jit_solution(6408804723810378223)
XLA Ops:
  2.1 8.7 %collective-permute-start = (f32[8,64,128]{2,1,0:T(8,128)S(1)}, f32[8,64,128]{2,1,0:T(8,128)S(1)}, u32[]{:S(2)}, u32[]{:S(2)}) collective-permute-start(f32[8,64,128]{2,1,0:T(8,128)S(1)} %fusion.50), channel_id=1, source_target_pairs={{0,4},{4,0},{8,12},{12,8},{16,20},{20,16},{24,28},{28,24},{32,36},... | collective-permute-start | bytes 786440 | tf_op jit(solution)/shard_map/ppermute | solution.py:31
  10.8 1.4 convolution_bitcast_fusion.7
  13.1 3.5 %all-to-all-start = ((f32[4,256,128]{2,1,0:T(8,128)}), f32[4,256,128]{2,1,0:T(8,128)S(1)}, u32[]{:S(2)}, u32[]{:S(2)}) async-start(f32[4,256,128]{2,1,0:T(8,128)} %bitcast.190), calls=%async_computation | async-start | bytes 1048576 | tf_op jit(solution)/shard_map/all_to_all | solution.py:24
  17.5 1.8 fusion.98
  21.4 1.9 collective-permute-start.1
  24.1 2.0 all-to-all-done
  26.9 3.3 %fusion.2 = f32[256,256,8]{1,2,0:T(8,128)S(1)} fusion(f32[256,8,16]{2,1,0:T(8,128)S(1)} %copy.184, s32[256,256]{1,0:T(8,128)S(1)} %convert_add_fusion, pred[256,256]{1,0:T(8,128)(4,1)S(1)} %iota_compare_fusion.1), kind=kOutput, calls=%fused_computation.2 | convolution fusion | flops 103809024 | bytes 2555904 | tf_op jit(solution)/shard_map/thl,lts->hts/dot_general | solution.py:87
  32.5 2.1 collective-permute-start.2
  34.7 6.2 %fusion = f32[256,8,16]{2,1,0:T(8,128)} fusion(f32[8,256,256]{2,1,0:T(8,128)S(1)} %get-tuple-element.58, s32[256,256]{1,0:T(8,128)S(1)} %copy-done.27, pred[256,256]{1,0:T(8,128)(4,1)S(1)} %copy-done.30), kind=kOutput, calls=%fused_computation | convolution fusion | flops 103809024 | bytes 2555904 | tf_op jit(solution)/shard_map/hts,lts->thl/dot_general | solution.py:99
  40.9 8.3 %collective-permute-done.2 = f32[8,64,128]{2,1,0:T(8,128)S(1)} collective-permute-done((f32[8,64,128]{2,1,0:T(8,128)S(1)}, f32[8,64,128]{2,1,0:T(8,128)S(1)}, u32[]{:S(2)}, u32[]{:S(2)}) %collective-permute-start.2) | collective-permute-done | bytes 262176 | tf_op jit(solution)/shard_map/ppermute | solution.py:31
  49.2 2.2 collective-permute-start.3
  51.4 1.4 convolution_bitcast_fusion.2
  52.9 12.5 %collective-permute-done.3 = f32[8,64,128]{2,1,0:T(8,128)S(1)} collective-permute-done((f32[8,64,128]{2,1,0:T(8,128)S(1)}, f32[8,64,128]{2,1,0:T(8,128)S(1)}, u32[]{:S(2)}, u32[]{:S(2)}) %collective-permute-start.3) | collective-permute-done | bytes 262176 | tf_op jit(solution)/shard_map/ppermute | solution.py:31
  66.1 1.9 collective-permute-start.4
  69.0 2.2 copy.198
  71.9 3.1 %collective-permute-done.4 = f32[8,64,128]{2,1,0:T(8,128)} collective-permute-done((f32[8,64,128]{2,1,0:T(8,128)}, f32[8,64,128]{2,1,0:T(8,128)}, u32[]{:S(2)}, u32[]{:S(2)}) %collective-permute-start.4) | collective-permute-done | bytes 262176 | tf_op jit(solution)/shard_map/ppermute | solution.py:31
  76.0 4.4 %collective-permute-start.5 = (f32[8,64,128]{2,1,0:T(8,128)S(1)}, f32[8,64,128]{2,1,0:T(8,128)S(1)}, u32[]{:S(2)}, u32[]{:S(2)}) collective-permute-start(f32[8,64,128]{2,1,0:T(8,128)S(1)} %add.179), channel_id=1, source_target_pairs={{0,128},{4,132},{8,136},{12,140},{16,144},{20,148},{24,152},{28,15... | collective-permute-start | bytes 786440 | tf_op jit(solution)/shard_map/ppermute | solution.py:31
  81.9 10.0 %collective-permute-done.5 = f32[8,64,128]{2,1,0:T(8,128)S(1)} collective-permute-done((f32[8,64,128]{2,1,0:T(8,128)S(1)}, f32[8,64,128]{2,1,0:T(8,128)S(1)}, u32[]{:S(2)}, u32[]{:S(2)}) %collective-permute-start.5) | collective-permute-done | bytes 262176 | tf_op jit(solution)/shard_map/ppermute | solution.py:31
  91.9 7.5 %collective-permute-start.6 = (f32[8,64,128]{2,1,0:T(8,128)S(1)}, f32[8,64,128]{2,1,0:T(8,128)S(1)}, u32[]{:S(2)}, u32[]{:S(2)}) collective-permute-start(f32[8,64,128]{2,1,0:T(8,128)S(1)} %add.180), channel_id=1, source_target_pairs={{0,256},{4,260},{8,264},{12,268},{16,272},{20,276},{24,280},{28,28... | collective-permute-start | bytes 786440 | tf_op jit(solution)/shard_map/ppermute | solution.py:31
  100.9 6.7 %collective-permute-done.6 = f32[8,64,128]{2,1,0:T(8,128)S(1)} collective-permute-done((f32[8,64,128]{2,1,0:T(8,128)S(1)}, f32[8,64,128]{2,1,0:T(8,128)S(1)}, u32[]{:S(2)}, u32[]{:S(2)}) %collective-permute-start.6) | collective-permute-done | bytes 262176 | tf_op jit(solution)/shard_map/ppermute | solution.py:31
  108.3 4.2 %fusion.8 = (f32[256,8,64]{0,2,1:T(8,128)}, f32[256,8,7,64]{0,3,2,1:T(8,128)S(1)}, f32[8,7,64,256]{3,2,1,0:T(8,128)S(1)}) fusion(f32[256,8,7]{0,2,1:T(8,128)S(1)} %copy-done.28, f32[256,8,64]{0,2,1:T(8,128)S(1)} %copy-done.9, bf16[256,8,128,1]{2,1,0,3:T(8,128)(2,1)S(1)} %bitcast.203, f32[7,8,64,128]{3,2,1,0:T(8,128)} %bitcast_dynamic-update-slice_fusion), kind=kOutput, calls=%fused_computation.9 | convolution fusion | flops 1411907584 | bytes 10805248 | tf_op jit(solution)/shard_map/thv,khdv->thkd/dot_general | solution.py:106
  112.5 1.9 fusion.26
  114.5 7.1 %collective-permute-start.7 = (f32[8,64,128]{2,1,0:T(8,128)S(1)}, f32[8,64,128]{2,1,0:T(8,128)S(1)}, u32[]{:S(2)}, u32[]{:S(2)}) collective-permute-start(f32[8,64,128]{2,1,0:T(8,128)S(1)} %fusion.73), channel_id=1, source_target_pairs={{0,256},{4,260},{8,264},{12,268},{16,272},{20,276},{24,280},{28,28... | collective-permute-start | bytes 786440 | tf_op jit(solution)/shard_map/ppermute | solution.py:31
  121.6 1.5 convolution_bitcast_fusion.3
  123.0 9.2 %collective-permute-done.7 = f32[8,64,128]{2,1,0:T(8,128)S(1)} collective-permute-done((f32[8,64,128]{2,1,0:T(8,128)S(1)}, f32[8,64,128]{2,1,0:T(8,128)S(1)}, u32[]{:S(2)}, u32[]{:S(2)}) %collective-permute-start.7) | collective-permute-done | bytes 262176 | tf_op jit(solution)/shard_map/ppermute | solution.py:31
  132.3 1.9 collective-permute-start.8
  135.3 13.3 %collective-permute-done.8 = f32[8,64,128]{2,1,0:T(8,128)S(1)} collective-permute-done((f32[8,64,128]{2,1,0:T(8,128)S(1)}, f32[8,64,128]{2,1,0:T(8,128)S(1)}, u32[]{:S(2)}, u32[]{:S(2)}) %collective-permute-start.8) | collective-permute-done | bytes 262176 | tf_op jit(solution)/shard_map/ppermute | solution.py:31
  148.6 2.1 collective-permute-start.9
  151.4 6.2 %collective-permute-done.9 = f32[8,64,128]{2,1,0:T(8,128)S(1)} collective-permute-done((f32[8,64,128]{2,1,0:T(8,128)S(1)}, f32[8,64,128]{2,1,0:T(8,128)S(1)}, u32[]{:S(2)}, u32[]{:S(2)}) %collective-permute-start.9) | collective-permute-done | bytes 262176 | tf_op jit(solution)/shard_map/ppermute | solution.py:31
  157.7 1.9 collective-permute-start.10
  161.0 8.3 %all-to-all-start.1 = ((bf16[4,256,128]{1,2,0:T(8,128)(2,1)}), bf16[4,256,128]{1,2,0:T(8,128)(2,1)S(1)}, u32[]{:S(2)}, u32[]{:S(2)}) async-start(bf16[4,256,128]{1,2,0:T(8,128)(2,1)} %broadcast_in_dim.54), calls=%async_computation.1 | async-start | bytes 524288 | tf_op jit(solution)/shard_map/all_to_all | solution.py:36
  169.2 4.0 %collective-permute-done.10 = f32[8,64,128]{2,1,0:T(8,128)S(1)} collective-permute-done((f32[8,64,128]{2,1,0:T(8,128)S(1)}, f32[8,64,128]{2,1,0:T(8,128)S(1)}, u32[]{:S(2)}, u32[]{:S(2)}) %collective-permute-start.10) | collective-permute-done | bytes 262176 | tf_op jit(solution)/shard_map/ppermute | solution.py:31
  173.2 1.8 fusion.65
  175.0 1.9 collective-permute-start.11
  177.7 1.3 convolution_bitcast_fusion
  179.0 1.5 reshape_reshape.3
  180.6 6.8 %all_to_all.20 = f32[2,64,4,512]{3,2,1,0:T(4,128)} all-to-all(f32[2,64,4,512]{3,2,1,0:T(4,128)S(1)} %bitcast.198), channel_id=1, replica_groups=mesh['seq_0'=8,'seq_1'=8,'seq_2'=2,'head'=4] {'seq_2'}, dimensions={0} | all-to-all | bytes 2097152 | tf_op jit(solution)/shard_map/all_to_all | solution.py:24
  187.4 2.5 %reduce_sum.31 = f32[64,4,512]{2,1,0:T(4,128)} reduce(f32[2,64,4,512]{3,2,1,0:T(4,128)} %all_to_all.20, f32[]{:T(128)} %constant.28.clone.1), dimensions={0}, to_apply=%region_1.2 | reduce | flops 131072 | bytes 1572868 | tf_op jit(solution)/shard_map/reduce_sum | solution.py:25
  189.9 8.1 %all-to-all-start.3 = ((f32[64,4,512]{2,1,0:T(4,128)}), f32[64,4,512]{2,1,0:T(4,128)}, u32[]{:S(2)}, u32[]{:S(2)}) async-start(f32[64,4,512]{2,1,0:T(4,128)} %reduce_sum.31), calls=%async_computation.3 | async-start | bytes 1048576 | tf_op jit(solution)/shard_map/all_to_all | solution.py:54
  199.3 3.0 %collective-permute-start.12 = (f32[8,64,128]{2,1,0:T(8,128)S(1)}, f32[8,64,128]{2,1,0:T(8,128)S(1)}, u32[]{:S(2)}, u32[]{:S(2)}) collective-permute-start(f32[8,64,128]{2,1,0:T(8,128)S(1)} %get-tuple-element.50), channel_id=1, source_target_pairs={{0,8},{4,12},{8,0},{12,4},{16,24},{20,28},{24,16},{28,20},{32,40},... | collective-permute-start | bytes 786440 | tf_op jit(solution)/shard_map/ppermute | solution.py:31
  202.3 6.7 %fusion.36 = bf16[256,8,128]{0,2,1:T(8,128)(2,1)} fusion(f32[256,8,128]{0,2,1:T(8,128)} %convolution_bitcast_fusion.3, f32[7,8,64,128]{3,2,1,0:T(8,128)S(1)} %copy-done.2, f32[256,8,7,64]{0,3,2,1:T(8,128)} %copy-done.1), kind=kOutput, calls=%fused_computation.38 | convolution fusion | flops 1409810432 | bytes 7077888 | tf_op jit(solution)/shard_map/thkd,khdv->thv/dot_general | solution.py:92
  208.9 6.8 %collective-permute-done.12 = f32[8,64,128]{2,1,0:T(8,128)S(1)} collective-permute-done((f32[8,64,128]{2,1,0:T(8,128)S(1)}, f32[8,64,128]{2,1,0:T(8,128)S(1)}, u32[]{:S(2)}, u32[]{:S(2)}) %collective-permute-start.12) | collective-permute-done | bytes 262176 | tf_op jit(solution)/shard_map/ppermute | solution.py:31
  215.8 1.7 fusion.61
  217.5 3.4 %collective-permute-start.13 = (f32[8,64,128]{2,1,0:T(8,128)}, f32[8,64,128]{2,1,0:T(8,128)}, u32[]{:S(2)}, u32[]{:S(2)}) collective-permute-start(f32[8,64,128]{2,1,0:T(8,128)} %get-tuple-element.48), channel_id=1, source_target_pairs={{0,4},{4,0},{8,12},{12,8},{16,20},{20,16},{24,28},{28,24},{32,36},... | collective-permute-start | bytes 786440 | tf_op jit(solution)/shard_map/ppermute | solution.py:31
  222.1 1.9 copy.204
  226.0 1.8 reduce_sum.32
  227.9 1.6 fusion.39
  230.5 1.6 fusion.43
  (114 shorter events, 26.5 us)
Async XLA Ops:
  0.6 1.2 copy-start
  1.8 15.8 %copy-start.6 = (bf16[256,512]{0,1:T(8,128)(2,1)}, bf16[256,512]{0,1:T(8,128)(2,1)S(1)}, u32[]{:S(2)}) copy-start(bf16[256,512]{0,1:T(8,128)(2,1)S(1)} %copy.180) | copy-start | bytes 786436
  1.8 14.7 %copy-start.25 = (bf16[256,512]{1,0:T(8,128)(2,1)S(1)}, bf16[256,512]{1,0:T(8,128)(2,1)}, u32[]{:S(2)}) copy-start(bf16[256,512]{1,0:T(8,128)(2,1)} %param.9) | copy-start | bytes 786436
  2.1 18.6 %collective-permute-start = (f32[8,64,128]{2,1,0:T(8,128)S(1)}, f32[8,64,128]{2,1,0:T(8,128)S(1)}, u32[]{:S(2)}, u32[]{:S(2)}) collective-permute-start(f32[8,64,128]{2,1,0:T(8,128)S(1)} %fusion.50), channel_id=1, source_target_pairs={{0,4},{4,0},{8,12},{12,8},{16,20},{20,16},{24,28},{28,24},{32,36},... | collective-permute-start | bytes 786440 | tf_op jit(solution)/shard_map/ppermute | solution.py:31
  13.1 13.0 %all-to-all-start = ((f32[4,256,128]{2,1,0:T(8,128)}), f32[4,256,128]{2,1,0:T(8,128)S(1)}, u32[]{:S(2)}, u32[]{:S(2)}) async-start(f32[4,256,128]{2,1,0:T(8,128)} %bitcast.190), calls=%async_computation | async-start | bytes 1048576 | tf_op jit(solution)/shard_map/all_to_all | solution.py:24
  16.6 2.9 %copy-start.3 = (bf16[256,1024]{1,0:T(8,128)(2,1)S(1)}, bf16[256,1024]{1,0:T(8,128)(2,1)}, u32[]{:S(2)}) copy-start(bf16[256,1024]{1,0:T(8,128)(2,1)} %param.12) | copy-start | bytes 1572868
  19.4 7.3 %copy-start.29 = (pred[256,256]{1,0:T(8,128)(4,1)}, pred[256,256]{1,0:T(8,128)(4,1)S(1)}, u32[]{:S(2)}) copy-start(pred[256,256]{1,0:T(8,128)(4,1)S(1)} %iota_compare_fusion.1) | copy-start | bytes 196612
  20.6 6.1 %copy-start.26 = (s32[256,256]{1,0:T(8,128)}, s32[256,256]{1,0:T(8,128)S(1)}, u32[]{:S(2)}) copy-start(s32[256,256]{1,0:T(8,128)S(1)} %convert_add_fusion) | copy-start | bytes 786436
  21.4 10.0 %collective-permute-start.1 = (f32[8,64,128]{2,1,0:T(8,128)}, f32[8,64,128]{2,1,0:T(8,128)}, u32[]{:S(2)}, u32[]{:S(2)}) collective-permute-start(f32[8,64,128]{2,1,0:T(8,128)} %add.175), channel_id=1, source_target_pairs={{0,8},{4,12},{8,0},{12,4},{16,24},{20,28},{24,16},{28,20},{32,40},... | collective-permute-start | bytes 786440 | tf_op jit(solution)/shard_map/ppermute | solution.py:31
  26.2 0.7 copy-start.23
  26.9 3.3 %copy-start.4 = (f32[8,256,256]{2,1,0:T(8,128)S(1)}, f32[8,256,256]{2,1,0:T(8,128)}, u32[]{:S(2)}) copy-start(f32[8,256,256]{2,1,0:T(8,128)} %fusion.98) | copy-start | bytes 6291460
  30.2 4.4 %copy-start.27 = (s32[256,256]{1,0:T(8,128)S(1)}, s32[256,256]{1,0:T(8,128)}, u32[]{:S(2)}) copy-start(s32[256,256]{1,0:T(8,128)} %copy-done.26) | copy-start | bytes 786436
  30.2 4.4 %copy-start.30 = (pred[256,256]{1,0:T(8,128)(4,1)S(1)}, pred[256,256]{1,0:T(8,128)(4,1)}, u32[]{:S(2)}) copy-start(pred[256,256]{1,0:T(8,128)(4,1)} %copy-done.29) | copy-start | bytes 196612
  32.5 16.6 %collective-permute-start.2 = (f32[8,64,128]{2,1,0:T(8,128)S(1)}, f32[8,64,128]{2,1,0:T(8,128)S(1)}, u32[]{:S(2)}, u32[]{:S(2)}) collective-permute-start(f32[8,64,128]{2,1,0:T(8,128)S(1)} %add.176), channel_id=1, source_target_pairs={{0,16},{4,20},{8,24},{12,28},{16,0},{20,4},{24,8},{28,12},{32,48},... | collective-permute-start | bytes 786440 | tf_op jit(solution)/shard_map/ppermute | solution.py:31
  40.9 27.1 %copy-start.24 = (f32[256,128]{0,1:T(8,128)S(1)}, f32[256,128]{0,1:T(8,128)}, u32[]{:S(2)}) copy-start(f32[256,128]{0,1:T(8,128)} %copy-done.23) | copy-start | bytes 393220
  49.2 17.0 %copy-start.19 = (f32[8,64,128]{2,1,0:T(8,128)}, f32[8,64,128]{2,1,0:T(8,128)S(1)}, u32[]{:S(2)}) copy-start(f32[8,64,128]{2,1,0:T(8,128)S(1)} %collective-permute-done.2) | copy-start | bytes 786436
  49.2 16.1 %collective-permute-start.3 = (f32[8,64,128]{2,1,0:T(8,128)S(1)}, f32[8,64,128]{2,1,0:T(8,128)S(1)}, u32[]{:S(2)}, u32[]{:S(2)}) collective-permute-start(f32[8,64,128]{2,1,0:T(8,128)S(1)} %add.177), channel_id=1, source_target_pairs={{0,32},{4,36},{8,40},{12,44},{16,48},{20,52},{24,56},{28,60},{32,0... | collective-permute-start | bytes 786440 | tf_op jit(solution)/shard_map/ppermute | solution.py:31
  65.3 2.7 %copy-start.20 = (f32[8,64,128]{2,1,0:T(8,128)}, f32[8,64,128]{2,1,0:T(8,128)S(1)}, u32[]{:S(2)}) copy-start(f32[8,64,128]{2,1,0:T(8,128)S(1)} %collective-permute-done.3) | copy-start | bytes 786436
  66.1 8.8 %collective-permute-start.4 = (f32[8,64,128]{2,1,0:T(8,128)}, f32[8,64,128]{2,1,0:T(8,128)}, u32[]{:S(2)}, u32[]{:S(2)}) collective-permute-start(f32[8,64,128]{2,1,0:T(8,128)} %add.178), channel_id=1, source_target_pairs={{0,64},{4,68},{8,72},{12,76},{16,80},{20,84},{24,88},{28,92},{32,9... | collective-permute-start | bytes 786440 | tf_op jit(solution)/shard_map/ppermute | solution.py:31
  71.9 36.4 %copy-start.9 = (f32[256,8,64]{0,2,1:T(8,128)S(1)}, f32[256,8,64]{0,2,1:T(8,128)}, u32[]{:S(2)}) copy-start(f32[256,8,64]{0,2,1:T(8,128)} %bitcast_convert_fusion) | copy-start | bytes 1572868
  71.9 36.4 %copy-start.17 = (bf16[32,8,8,128]{3,2,1,0:T(8,128)(2,1)S(1)}, bf16[32,8,8,128]{3,2,1,0:T(8,128)(2,1)}, u32[]{:S(2)}) copy-start(bf16[32,8,8,128]{3,2,1,0:T(8,128)(2,1)} %copy.229) | copy-start | bytes 1572868
  71.9 36.4 %copy-start.28 = (f32[256,8,7]{0,2,1:T(8,128)S(1)}, f32[256,8,7]{0,2,1:T(8,128)}, u32[]{:S(2)}) copy-start(f32[256,8,7]{0,2,1:T(8,128)} %fusion.78) | copy-start | bytes 172036
  76.0 15.9 %collective-permute-start.5 = (f32[8,64,128]{2,1,0:T(8,128)S(1)}, f32[8,64,128]{2,1,0:T(8,128)S(1)}, u32[]{:S(2)}, u32[]{:S(2)}) collective-permute-start(f32[8,64,128]{2,1,0:T(8,128)S(1)} %add.179), channel_id=1, source_target_pairs={{0,128},{4,132},{8,136},{12,140},{16,144},{20,148},{24,152},{28,15... | collective-permute-start | bytes 786440 | tf_op jit(solution)/shard_map/ppermute | solution.py:31
  91.9 15.7 %collective-permute-start.6 = (f32[8,64,128]{2,1,0:T(8,128)S(1)}, f32[8,64,128]{2,1,0:T(8,128)S(1)}, u32[]{:S(2)}, u32[]{:S(2)}) collective-permute-start(f32[8,64,128]{2,1,0:T(8,128)S(1)} %add.180), channel_id=1, source_target_pairs={{0,256},{4,260},{8,264},{12,268},{16,272},{20,276},{24,280},{28,28... | collective-permute-start | bytes 786440 | tf_op jit(solution)/shard_map/ppermute | solution.py:31
  112.5 1.9 copy-start.1
  112.5 1.9 copy-start.11
  114.4 43.2 %copy-start.5 = (f32[7,8,64,128]{3,2,1,0:T(8,128)}, f32[7,8,64,128]{3,2,1,0:T(8,128)S(1)}, u32[]{:S(2)}) copy-start(f32[7,8,64,128]{3,2,1,0:T(8,128)S(1)} %fusion.26) | copy-start | bytes 5505028
  114.5 17.7 %collective-permute-start.7 = (f32[8,64,128]{2,1,0:T(8,128)S(1)}, f32[8,64,128]{2,1,0:T(8,128)S(1)}, u32[]{:S(2)}, u32[]{:S(2)}) collective-permute-start(f32[8,64,128]{2,1,0:T(8,128)S(1)} %fusion.73), channel_id=1, source_target_pairs={{0,256},{4,260},{8,264},{12,268},{16,272},{20,276},{24,280},{28,28... | collective-permute-start | bytes 786440 | tf_op jit(solution)/shard_map/ppermute | solution.py:31
  132.3 16.3 %collective-permute-start.8 = (f32[8,64,128]{2,1,0:T(8,128)S(1)}, f32[8,64,128]{2,1,0:T(8,128)S(1)}, u32[]{:S(2)}, u32[]{:S(2)}) collective-permute-start(f32[8,64,128]{2,1,0:T(8,128)S(1)} %fusion.71), channel_id=1, source_target_pairs={{0,128},{4,132},{8,136},{12,140},{16,144},{20,148},{24,152},{28,15... | collective-permute-start | bytes 786440 | tf_op jit(solution)/shard_map/ppermute | solution.py:31
  148.6 8.9 %collective-permute-start.9 = (f32[8,64,128]{2,1,0:T(8,128)S(1)}, f32[8,64,128]{2,1,0:T(8,128)S(1)}, u32[]{:S(2)}, u32[]{:S(2)}) collective-permute-start(f32[8,64,128]{2,1,0:T(8,128)S(1)} %get-tuple-element.56), channel_id=1, source_target_pairs={{0,64},{4,68},{8,72},{12,76},{16,80},{20,84},{24,88},{28,92},{32,9... | collective-permute-start | bytes 786440 | tf_op jit(solution)/shard_map/ppermute | solution.py:31
  150.8 8.8 %copy-start.22 = (f32[256,8,16]{0,2,1:T(8,128)S(1)}, f32[256,8,16]{0,2,1:T(8,128)}, u32[]{:S(2)}) copy-start(f32[256,8,16]{0,2,1:T(8,128)} %copy.198) | copy-start | bytes 393220
  157.6 20.1 %copy-start.21 = (bf16[256,512]{1,0:T(8,128)(2,1)S(1)}, bf16[256,512]{1,0:T(8,128)(2,1)}, u32[]{:S(2)}) copy-start(bf16[256,512]{1,0:T(8,128)(2,1)} %param.7) | copy-start | bytes 786436
  157.7 15.6 %collective-permute-start.10 = (f32[8,64,128]{2,1,0:T(8,128)S(1)}, f32[8,64,128]{2,1,0:T(8,128)S(1)}, u32[]{:S(2)}, u32[]{:S(2)}) collective-permute-start(f32[8,64,128]{2,1,0:T(8,128)S(1)} %get-tuple-element.54), channel_id=1, source_target_pairs={{0,32},{4,36},{8,40},{12,44},{16,48},{20,52},{24,56},{28,60},{32,0... | collective-permute-start | bytes 786440 | tf_op jit(solution)/shard_map/ppermute | solution.py:31
  161.0 16.0 %all-to-all-start.1 = ((bf16[4,256,128]{1,2,0:T(8,128)(2,1)}), bf16[4,256,128]{1,2,0:T(8,128)(2,1)S(1)}, u32[]{:S(2)}, u32[]{:S(2)}) async-start(bf16[4,256,128]{1,2,0:T(8,128)(2,1)} %broadcast_in_dim.54), calls=%async_computation.1 | async-start | bytes 524288 | tf_op jit(solution)/shard_map/all_to_all | solution.py:36
  175.0 23.0 %collective-permute-start.11 = (f32[8,64,128]{2,1,0:T(8,128)}, f32[8,64,128]{2,1,0:T(8,128)}, u32[]{:S(2)}, u32[]{:S(2)}) collective-permute-start(f32[8,64,128]{2,1,0:T(8,128)} %get-tuple-element.52), channel_id=1, source_target_pairs={{0,16},{4,20},{8,24},{12,28},{16,0},{20,4},{24,8},{28,12},{32,48},... | collective-permute-start | bytes 786440 | tf_op jit(solution)/shard_map/ppermute | solution.py:31
  177.0 0.7 copy-start.12
  187.4 14.9 %copy-start.2 = (f32[7,8,64,128]{3,2,1,0:T(8,128)S(1)}, f32[7,8,64,128]{3,2,1,0:T(8,128)}, u32[]{:S(2)}) copy-start(f32[7,8,64,128]{3,2,1,0:T(8,128)} %bitcast_dynamic-update-slice_fusion) | copy-start | bytes 5505028
  189.9 36.1 %all-to-all-start.3 = ((f32[64,4,512]{2,1,0:T(4,128)}), f32[64,4,512]{2,1,0:T(4,128)}, u32[]{:S(2)}, u32[]{:S(2)}) async-start(f32[64,4,512]{2,1,0:T(4,128)} %reduce_sum.31), calls=%async_computation.3 | async-start | bytes 1048576 | tf_op jit(solution)/shard_map/all_to_all | solution.py:54
  199.2 21.7 %copy-start.7 = (bf16[256,512]{0,1:T(8,128)(2,1)S(1)}, bf16[256,512]{0,1:T(8,128)(2,1)}, u32[]{:S(2)}) copy-start(bf16[256,512]{0,1:T(8,128)(2,1)} %copy-done.6) | copy-start | bytes 786436
  199.3 21.7 %copy-start.18 = (f32[256,8,64]{0,2,1:T(8,128)S(1)}, f32[256,8,64]{0,2,1:T(8,128)}, u32[]{:S(2)}) copy-start(f32[256,8,64]{0,2,1:T(8,128)} %get-tuple-element.61) | copy-start | bytes 1572868
  199.3 16.5 %collective-permute-start.12 = (f32[8,64,128]{2,1,0:T(8,128)S(1)}, f32[8,64,128]{2,1,0:T(8,128)S(1)}, u32[]{:S(2)}, u32[]{:S(2)}) collective-permute-start(f32[8,64,128]{2,1,0:T(8,128)S(1)} %get-tuple-element.50), channel_id=1, source_target_pairs={{0,8},{4,12},{8,0},{12,4},{16,24},{20,28},{24,16},{28,20},{32,40},... | collective-permute-start | bytes 786440 | tf_op jit(solution)/shard_map/ppermute | solution.py:31
  208.9 15.0 %copy-start.15 = (bf16[256,8,128]{0,2,1:T(8,128)(2,1)S(1)}, bf16[256,8,128]{0,2,1:T(8,128)(2,1)}, u32[]{:S(2)}) copy-start(bf16[256,8,128]{0,2,1:T(8,128)(2,1)} %fusion.36) | copy-start | bytes 1572868
  217.5 7.5 %copy-start.13 = (bf16[4,256,128]{1,2,0:T(8,128)(2,1)S(1)}, bf16[4,256,128]{1,2,0:T(8,128)(2,1)}, u32[]{:S(2)}) copy-start(bf16[4,256,128]{1,2,0:T(8,128)(2,1)} %copy-done.12) | copy-start | bytes 786436
  217.5 7.5 %copy-start.16 = (bf16[512,512]{1,0:T(8,128)(2,1)S(1)}, bf16[512,512]{1,0:T(8,128)(2,1)}, u32[]{:S(2)}) copy-start(bf16[512,512]{1,0:T(8,128)(2,1)} %param.8) | copy-start | bytes 1572868
  217.5 10.4 %collective-permute-start.13 = (f32[8,64,128]{2,1,0:T(8,128)}, f32[8,64,128]{2,1,0:T(8,128)}, u32[]{:S(2)}, u32[]{:S(2)}) collective-permute-start(f32[8,64,128]{2,1,0:T(8,128)} %get-tuple-element.48), channel_id=1, source_target_pairs={{0,4},{4,0},{8,12},{12,8},{16,20},{20,16},{24,28},{28,24},{32,36},... | collective-permute-start | bytes 786440 | tf_op jit(solution)/shard_map/ppermute | solution.py:31
  222.1 5.8 %copy-start.8 = (bf16[256,512]{0,1:T(8,128)(2,1)S(1)}, bf16[256,512]{0,1:T(8,128)(2,1)}, u32[]{:S(2)}) copy-start(bf16[256,512]{0,1:T(8,128)(2,1)} %copy-done.6) | copy-start | bytes 786436
  222.1 5.8 %copy-start.10 = (f32[256,8,128]{0,2,1:T(8,128)S(1)}, f32[256,8,128]{0,2,1:T(8,128)}, u32[]{:S(2)}) copy-start(f32[256,8,128]{0,2,1:T(8,128)} %convolution_bitcast_fusion.2) | copy-start | bytes 3145732
  226.0 4.4 %copy-start.14 = (f32[256,8,64]{0,2,1:T(8,128)S(1)}, f32[256,8,64]{0,2,1:T(8,128)}, u32[]{:S(2)}) copy-start(f32[256,8,64]{0,2,1:T(8,128)} %convolution_bitcast_fusion.4) | copy-start | bytes 1572868
where the time goes:
time: 234 us; the launch traced here: 233 us
  waiting for transfers between devices  82.1 us (35%)
  starting transfers between devices  70 us (30%)
  matrix products  38.9 us (17%)
  other arithmetic  19.9 us (9%)
  local copies, waits for them, and re-layouts  13.9 us (6%)
  blocking collectives  6.78 us (3%)
    ppermute x14, waiting for transfers between devices, partner_2(): return lax.ppermute(value, axis, pairs)  80.1 us
    ppermute x14, starting transfers between devices, partner_2(): return lax.ppermute(value, axis, pairs)  50.1 us
    all_to_all x1, starting transfers between devices, copy_for_each(): return lax.all_to_all(copies, axis, split_axis=0, concat_axis=0, tiled=True)  8.25 us
    all_to_all x1, starting transfers between devices, sum_by_axis(): lax.all_to_all(nearer, far, split_axis=0, concat_axis=0, tiled=True)  8.15 us
    unnamed x69, local copies, waits for them, and re-layouts  7.88 us
    all_to_all x1, blocking collectives, summed_on_arrival(): lax.all_to_all(pieces, axis, split_axis=0, concat_axis=0, tiled=True)  6.78 us
    dot_general x1, matrix products, local_pass(): carried = jnp.einsum('thkd,khdv->thv', scaled, states, precision=PRECISE)  6.68 us
    dot_general x1, matrix products, local_pass(): jnp.einsum('hts,lts->thl', grad_mixed * scores, table, precision=PRECISE)  6.23 us
  transfers between devices with their start and end apart: 17, of which 12 were waited for; matrix products, arithmetic and copies ran while one was open for 24% of the time, Pallas kernels for 0%

commit v1 on v0

v1 whole, which is shorter than its diff:
```python
import functools

import jax
import jax.numpy as jnp
import numpy as np
from jax import lax
from jax.experimental import pallas as pl
from jax.experimental.pallas import tpu as pltpu
from jax.sharding import PartitionSpec as P

DK = 64
DV = 128
LEVELS = 16
BASE = 9
T = 256
F32 = jnp.float32
BF16 = jnp.bfloat16


def dot(a, b, da, db):
    return lax.dot_general(a, b, (((da,), (db,)), ((), ())), preferred_element_type=F32)


def mm(a, b):
    return dot(a, b, 1, 0)


def segment_tables():
    select = np.zeros((128, 256), np.float32)
    member = np.zeros((256, 128), np.float32)
    level = np.full((256,), 99, np.int32)
    level[:128] = 0
    rows = np.arange(128)
    select[rows, rows] = 1.0
    member[rows, rows] = 1.0
    col = 128
    for k in range(7):
        for i in range(64 >> k):
            select[:, col] = (rows >> k) == 2 * i + 1
            member[col, :] = (rows >> k) == 2 * i
            level[col] = k + 1
            col += 1
    return np.concatenate([select, select], 0), member, level


class Sems:
    def __init__(self, send, recv):
        self.send, self.recv, self.used = send, recv, 0

    def take(self):
        at = self.used
        self.used += 1
        return (None if self.send is None else (self.send.at[at], self.recv.at[at]))


def kernel(cfg, *refs):
    nz, ny, nx, ly, lz = cfg
    nl = 1 + ly + lz
    ch = T // ny
    nq = nx // 2
    rz = 512 // nz
    ry = rz // ny
    names = (
        "in0", "in1", "in2", "in3", "in4", "in5", "in6", "in7", "in8", "in9", "o_out", "o_dq", "o_dk", "o_dv", "o_dh", "o_dw",
        "part", "rX", "kv", "kvf", "pk", "S", "rB", "tY", "TT", "rC", "UZ", "U", "sQ", "lw2", "G", "Gf", "pG", "GS",
        "rD", "GZ", "rC2", "R", "adj", "oacc", "dq", "dk", "dv", "gl", "sig", "lwb", "gpA", "dws", "rDW", "dw0a", "rd0a", "dw1a", "rd1a",
        "dw0b", "rd0b", "dw1b", "rd1b",  "hid", "w", "q", "k", "v", "g", "dst", "sel", "mem", "lev",
        "scs", "gms", "hidp", "send", "recv", "load",
    )
    r = dict(zip(names, refs, strict=True))
    hid, w, q, k, v, g = (r[n] for n in ("hid", "w", "q", "k", "v", "g"))
    sems = Sems(r["send"], r["recv"])

    s = lax.axis_index("seq")
    x = lax.axis_index("head")
    c = s % 2
    y = (s // 2) % ny
    z = s // (2 * ny)

    def dev(zz, yy, cc, xx):
        return (zz * (2 * ny) + yy * 2 + cc, xx)

    def rc(src, dst, sem, to):
        return pltpu.make_async_remote_copy(
            src_ref=src, dst_ref=dst, send_sem=sem[0], recv_sem=sem[1], device_id=to,
            device_id_type=pl.DeviceIdType.MESH,
        )

    partner = dev(z, y, 1 - c, x)
    y_order = sorted(range(1, ny), key=lambda d: -min(d, ny - d))
    z_order = sorted(range(1, nz), key=lambda d: -min(d, nz - d))
    x_order = sorted(range(1, nx), key=lambda d: -min(d, nx - d))
    pending = []

    def arrive(ref, sem):
        rc(ref, ref, sem, partner).wait_recv()

    def leave(ref, sem, cond=None):
        pending.append((cond, rc(ref, ref, sem, partner)))

    def chunks(n):
        return r["rB"].at[pl.ds(0, n)]

    def when(cond, action):
        if cond is None:
            action()
        else:
            pl.when(cond)(action)

    def bit(value, j):
        return (value // (1 << j)) % 2

    def rows(at, count):
        return pl.ds(pl.multiple_of(at * count, count), count)

    arrays = ("hid", "w", "q", "k", "v", "g", "dst", "sel", "mem", "lev")
    loads = {n: pltpu.make_async_copy(r[f"in{i}"], r[n], r["load"].at[i]) for i, n in enumerate(arrays)}

    def loaded(*wanted):
        for n in wanted:
            loads[n].wait()

    U, G, pG = r["U"], r["G"], r["pG"]
    barrier = pltpu.get_barrier_semaphore()
    peers = [partner]
    peers += [dev(z, y, c, (x + d) % nx) for d in x_order]
    for t in (c, 1 - c):
        peers += [dev(z, (y + d) % ny, t, x) for d in y_order]
        peers += [dev((z + d) % nz, y, t, x) for d in z_order]
    for peer in peers:
        pl.semaphore_signal(barrier, inc=1, device_id=peer, device_id_type=pl.DeviceIdType.MESH)
    for n in ("k", "v", "hid", "w", "q", "g", "mem", "sel", "lev", "dst"):
        loads[n].start()
    for level in range(nl):
        U[level] = jnp.zeros((512, 128), BF16)

    lane = lax.broadcasted_iota(jnp.int32, (1, 128), 1)
    low = lane < DK

    def pair_rows(full):
        return jnp.concatenate([full[:DK, :128], full[DK:, 128:]], 0)

    def spread_pair(block):
        zero = jnp.zeros((DK, 128), block.dtype)
        left = jnp.concatenate([block[:DK], zero], 0)
        right = jnp.concatenate([zero, block[DK:]], 0)
        return jnp.concatenate([left, right], 1)

    def l128(p):
        return pl.ds(pl.multiple_of(p * 128, 128), 128)

    def l256(p):
        return pl.ds(pl.multiple_of(p * 256, 256), 256)

    loaded("k", "v")
    for p in range(4):
        full = dot(k[:, l128(p)], v[:, l256(p)], 0, 0)
        state = pair_rows(full)
        r["kvf"][pl.ds(p * 128, 128), :] = state
        r["kv"][pl.ds(p * 128, 128), :] = state.astype(BF16)
    loaded("hid", "w")
    for j in range(nx):
        r["part"][j] = mm(hid[...], w[:, pl.ds(j * 128, 128)])

    pl.semaphore_wait(barrier, len(peers))

    a_copy = rc(r["kv"], r["pk"], sems.take(), partner)
    a_copy.start()
    pending.append((None, a_copy))
    x_sem = sems.take()
    for d in x_order:
        to = (x + d) % nx
        rc(r["part"].at[to], r["rX"].at[x], x_sem, dev(z, y, c, to)).start()
    leave(r["part"].at[0:nx - 1], x_sem)

    src = lax.broadcasted_iota(jnp.int32, (512, 512), 0)
    col = lax.broadcasted_iota(jnp.int32, (512, 512), 1)
    wanted = ((col // ry) % nz) * rz + (col // (nz * ry)) * ry + col % ry
    r["hidp"][...] = mm(hid[...], jnp.where(src == wanted, 1.0, 0.0).astype(BF16)).astype(BF16)

    a_copy.wait_recv()
    half = rows(c, T)
    mine = r["kvf"][half, :] + r["pk"][half, :].astype(F32)
    r["S"][...] = mine.astype(BF16)
    U[0] = (r["pk"][...].astype(F32) * c.astype(F32)).astype(BF16)
    b_sem = sems.take()
    for d in y_order:
        to = (y + d) % ny
        rc(r["S"].at[rows(to, ch)], r["rB"].at[y], b_sem, dev(z, to, c, x)).start()
    leave(chunks(ny - 1), b_sem)
    r["rB"][y] = r["S"][rows(y, ch), :]

    loaded("q", "g", "mem", "sel", "lev")
    head_row = lax.broadcasted_iota(jnp.int32, (128, 384), 0)

    def level_columns(head):
        return jnp.where(head_row == head * LEVELS + r["lev"][...], 1.0, 0.0).astype(BF16)

    def split_in_two(value):
        upper_part = value.astype(BF16)
        return jnp.concatenate([upper_part, (value - upper_part.astype(F32)).astype(BF16)], 1)

    def scores(p, carry):
        q2 = q[:, l128(p)]
        k2 = k[:, l128(p)]
        member = r["mem"][...]
        gl = r["gl"][...]
        for i in range(2):
            mask = low if i == 0 else jnp.logical_not(low)
            qh = jnp.where(mask, q2, jnp.zeros_like(q2))
            at = pl.ds(pl.multiple_of(p * 256 + i * 128, 128), 128)
            sc = dot(qh, k2, 1, 1)
            gm = dot(g[:, at], v[:, at], 1, 1)
            sc = jnp.concatenate([sc[:128, :128], sc[128:, 128:], sc[128:, :128]], 0)
            gm = jnp.concatenate([gm[:128, :128], gm[128:, 128:], gm[128:, :128]], 0)
            r["scs"][2 * p + i] = sc
            r["gms"][2 * p + i] = gm
            table = level_columns(2 * p + i)
            prod = split_in_two(sc * gm)
            near = dot(prod[:256], jnp.concatenate([member, member], 1), 1, 1)
            near = near.astype(BF16) * r["sel"][...]
            gl = gl + dot(near, table[:, :256], 1, 1)
            far = dot(prod[256:], jnp.concatenate([table[:, 256:], table[:, 256:]], 1), 1, 1)
            gl = gl + jnp.concatenate([jnp.zeros((128, 128), F32), far], 0)
        r["gl"][...] = gl
        return carry

    r["gl"][...] = jnp.zeros((T, 128), F32)
    lax.fori_loop(0, 4, scores, 0)

    arrive(chunks(ny - 1), b_sem)
    sums = [r["rB"][i].astype(F32) for i in range(ny)]
    for j in range(1, ly):
        sums = [sums[2 * i] + sums[2 * i + 1] for i in range(len(sums) // 2)]
        for i, value in enumerate(sums):
            r["tY"][j, i] = value.astype(BF16)
    r["TT"][...] = (sums[0] + sums[1]).astype(BF16)
    c_sem = sems.take()
    for d in range(nz - 1, 0, -1):
        to = (z + d) % nz
        cp = rc(r["TT"], r["rC"].at[z], c_sem, dev(to, y, c, x))
        when(z + d < nz, cp.start)
    for at in range(nz - 1):
        leave(r["rC"].at[0:nz - 1 - at], c_sem, z == at)

    def y_source(level, target):
        at = target // (1 << level) - 1
        at = (at + ny) % ny
        return r["rB"].at[at] if level == 0 else r["tY"].at[level, at]

    slot = c * ny + y
    d_sems = [sems.take() for _ in range(ly + lz)]
    for level in range(ly):
        for d in y_order:
            to = (y + d) % ny
            cp = rc(
                y_source(level, to), U.at[1 + level, rows(slot, ch)], d_sems[level], dev(z, to, c, x)
            )
            when(bit(to, level) == 1, cp.start)
        for own in range(2):
            if ny // 2 - own:
                leave(chunks(ny // 2 - own), d_sems[level], bit(y, level) == own)

        @pl.when(bit(y, level) == 1)
        def _():
            U[1 + level, rows(slot, ch), :] = y_source(level, y)[...]

    arrive(r["rX"].at[0:nx - 1], x_sem)
    r["rX"][x] = r["part"][x]
    projected = r["rX"][0]
    for j in range(1, nx):
        projected = projected + r["rX"][j]
    weights = jnp.maximum(projected, 0.0) + jnp.log1p(jnp.exp(-jnp.abs(projected)))
    upper_part = weights.astype(BF16)
    rest = (weights - upper_part.astype(F32)).astype(BF16)
    r["lwb"][...] = jnp.concatenate([upper_part, rest], 1)
    r["sig"][...] = jax.nn.sigmoid(projected)

    row_id = lax.broadcasted_iota(jnp.int32, (128, nl * 128), 0)
    col_id = lax.broadcasted_iota(jnp.int32, (128, nl * 128), 1)
    col_level = BASE + col_id // 128
    col_head = (col_id % 128) // DK

    def upper_table(p):
        return jnp.where(row_id == (2 * p + col_head) * LEVELS + col_level, 1.0, 0.0).astype(BF16)

    def grad_states(p, carry):
        table = upper_table(p)
        wide = mm(r["lwb"][...], jnp.concatenate([table, table], 0))
        r["lw2"][p] = wide.astype(BF16)
        q2 = q[:, l128(p)].astype(F32)
        gg = g[:, l256(p)]
        for m in range(nl):
            scaled = (wide[:, m * 128:(m + 1) * 128] * q2).astype(BF16)
            r["sQ"][p, :, m * 128:(m + 1) * 128] = scaled
            state = pair_rows(dot(scaled, gg, 0, 0))
            r["Gf"][m, rows(p, 128), :] = state
            G[m, rows(p, 128), :] = state.astype(BF16)
        return carry

    lax.fori_loop(0, 4, grad_states, 0)
    ga = rc(G.at[0], pG.at[0], sems.take(), partner)
    ga.start()
    pending.append((None, ga))
    other = rows(1 - c, T)
    gb = rc(G.at[1:nl, other], pG.at[1:nl, other], sems.take(), partner)
    gb.start()
    pending.append((None, gb))

    def local_pair(p, carry):
        q2 = q[:, l128(p)]
        k2 = k[:, l128(p)]
        select = r["sel"][...]
        member = r["mem"][...]
        dq2 = jnp.zeros((T, 128), F32)
        dk2 = jnp.zeros((T, 128), F32)
        zero = jnp.zeros((128, 128), BF16)
        for i in range(2):
            mask = low if i == 0 else jnp.logical_not(low)
            qh = jnp.where(mask, q2, jnp.zeros_like(q2))
            kh = jnp.where(mask, k2, jnp.zeros_like(k2))
            at = pl.ds(pl.multiple_of(p * 256 + i * 128, 128), 128)
            vh = v[:, at]
            gh = g[:, at]
            table = level_columns(2 * p + i)
            wide = mm(r["lwb"][...], jnp.concatenate([table, table], 0))
            chosen = wide[:, :256].astype(BF16) * select
            spread = mm(chosen, member)
            far = wide[128:, 256:]
            both = jnp.concatenate([spread, far], 0)
            mixed = (r["scs"][2 * p + i] * both).astype(BF16)
            gs = (r["gms"][2 * p + i] * both).astype(BF16)

            def square(block):
                top = jnp.concatenate([block[:128], zero], 1)
                return jnp.concatenate([top, jnp.concatenate([block[256:], block[128:256]], 1)], 0)

            mixed = square(mixed)
            gs = square(gs)
            r["oacc"][:, at] = mm(mixed, vh)
            r["dv"][:, at] = dot(mixed, gh, 0, 0)
            dq2 = dq2 + mm(gs, kh)
            dk2 = dk2 + dot(gs, qh, 0, 0)
        r["dq"][:, l128(p)] = dq2
        r["dk"][:, l128(p)] = dk2
        return carry

    lax.fori_loop(0, 1, local_pair, 0)

    for at in range(1, nz):
        when(z == at, rc(r["rC"].at[0:at], r["rC"].at[0:at], c_sem, partner).wait_recv)
    for level in range(lz):
        @pl.when(bit(z, level) == 1)
        def _():
            start = (z // (1 << level) - 1) * (1 << level)
            value = r["rC"][start].astype(F32)
            for i in range(1, 1 << level):
                value = value + r["rC"][start + i].astype(F32)
            r["UZ"][level] = value.astype(BF16)
            for d in y_order:
                to = (y + d) % ny
                rc(
                    r["UZ"].at[level], U.at[1 + ly + level, rows(slot, ch)], d_sems[ly + level], dev(z, to, c, x)
                ).start()
            U[1 + ly + level, rows(slot, ch), :] = r["UZ"][level]
        leave(chunks(ny - 1), d_sems[ly + level], bit(z, level) == 1)

    def shared(first, last):
        for level in range(first, last):
            own_bit = bit(y, level) if level < ly else bit(z, level - ly)
            when(own_bit == 1, rc(chunks(ny - 1), chunks(ny - 1), d_sems[level], partner).wait_recv)
        part = U.at[1 + first:1 + last, half]
        cp = rc(part, part, sems.take(), partner)
        cp.start()
        pending.append((None, cp))
        return cp

    share_y = shared(0, ly)

    gb.wait_recv()
    for level in range(ly + lz):
        both = r["Gf"][1 + level, half, :] + pG[1 + level, half, :].astype(F32)
        r["GS"][level] = both.astype(BF16)
    e_sems = [sems.take() for _ in range(ly + lz)]
    for level in range(ly + lz):
        own_bit = bit(y, level) if level < ly else bit(z, level - ly)
        leave(chunks(ny - 1), e_sems[level], own_bit == 1)

        @pl.when(own_bit == 1)
        def _():
            for d in y_order:
                to = (y + d) % ny
                rc(
                    r["GS"].at[level, rows(to, ch)], r["rD"].at[y, level], e_sems[level], dev(z, to, c, x)
                ).start()
            r["rD"][y, level] = r["GS"][level, rows(y, ch), :]

    lax.fori_loop(1, 4, local_pair, 0)

    def states_of(p, first, last):
        return jnp.concatenate([spread_pair(U[m, rows(p, 128), :]) for m in range(first, last)], 0)

    def add_levels(p, back, first, last):
        count = last - first
        q2 = q[:, l128(p)].astype(F32)
        terms = [split_in_two(back[:, m * 128:(m + 1) * 128] * q2) for m in range(count)]
        out_row = lax.broadcasted_iota(jnp.int32, (count * 256, 128), 0)
        out_col = lax.broadcasted_iota(jnp.int32, (count * 256, 128), 1)
        table = jnp.where(
            out_col == (2 * p + (out_row % 128) // DK) * LEVELS + BASE + first + out_row // 256, 1.0, 0.0
        ).astype(BF16)
        r["gl"][...] += mm(jnp.concatenate(terms, 1), table)

    def add_states(p, back, wide, first, last):
        columns = slice(first * 128, last * 128)
        out = r["oacc"][:, l256(p)] + mm(r["sQ"][p, :, columns], wide)
        dq2 = r["dq"][:, l128(p)]
        for m in range(last - first):
            at = slice((first + m) * 128, (first + m + 1) * 128)
            dq2 = dq2 + r["lw2"][p, :, at].astype(F32) * back[:, m * 128:(m + 1) * 128]
        return out, dq2

    def near_levels(p, carry):
        wide = states_of(p, 0, 1 + ly)
        back = dot(g[:, l256(p)], wide, 1, 1)
        add_levels(p, back, 0, 1 + ly)
        out, dq2 = add_states(p, back, wide, 0, 1 + ly)
        r["oacc"][:, l256(p)] = out
        r["dq"][:, l128(p)] = dq2
        return carry

    def far_levels(p, carry):
        add_levels(p, dot(g[:, l256(p)], states_of(p, 1 + ly, nl), 1, 1), 1 + ly, nl)
        return carry

    def far_states(p, carry):
        wide = states_of(p, 1 + ly, nl)
        out, dq2 = add_states(p, dot(g[:, l256(p)], wide, 1, 1), wide, 1 + ly, nl)
        r["o_out"][:, l256(p)] = out.astype(BF16)
        r["o_dq"][:, l128(p)] = dq2.astype(BF16)
        return carry

    share_y.wait_recv()
    lax.fori_loop(0, 4, near_levels, 0)
    share_z = shared(ly, ly + lz)
    share_z.wait_recv()
    lax.fori_loop(0, 4, far_levels, 0)
    gp = (r["gl"][...] * r["sig"][...]).astype(BF16)
    r["gpA"][x] = gp
    g_sem = sems.take()
    for d in x_order:
        to = (x + d) % nx
        rc(r["gpA"].at[x], r["gpA"].at[x], g_sem, dev(z, y, c, to)).start()
    leave(r["gpA"].at[0:nx - 1], g_sem)

    lax.fori_loop(0, 4, far_states, 0)

    for level in range(ly + lz):
        if level >= ly:
            when(bit(z, level - ly) == 1, rc(chunks(ny - 1), chunks(ny - 1), e_sems[level], partner).wait_recv)
            continue
        for own in range(2):
            n = ny // 2 - own
            if n:
                when(bit(y, level) == own, rc(chunks(n), chunks(n), e_sems[level], partner).wait_recv)
    for level in range(lz):
        @pl.when(bit(z, level) == 1)
        def _():
            value = r["rD"][0, ly + level].astype(F32)
            for i in range(1, ny):
                value = value + r["rD"][i, ly + level].astype(F32)
            r["GZ"][level] = value.astype(BF16)
    f_sem = sems.take()
    for d in range(nz - 1, 0, -1):
        to = (z + nz - d) % nz
        top = 0
        for level in range(lz):
            apart = z // (1 << level) - to // (1 << level)
            top = top + (apart + nz - 1) // nz
        at = (top + lz - 1) % lz
        cp = rc(r["GZ"].at[at], r["rC2"].at[z], f_sem, dev(to, y, c, x))
        when(z >= d, cp.start)
    for at in range(1, nz):
        leave(r["rC2"].at[0:at], f_sem, z == at)

    arrive(r["gpA"].at[0:nx - 1], g_sem)
    def left(j):
        return hid[...] if j % 2 == 0 else r["hidp"][...]

    for j in range(nq):
        r["dws"][j] = dot(left(j), r["gpA"][(1 - c) * nq + j], 0, 0).astype(BF16)
    w_copy = rc(r["dws"], r["rDW"], sems.take(), partner)
    w_copy.start()
    pending.append((None, w_copy))
    own_dw = [dot(left(j), r["gpA"][c * nq + j], 0, 0) for j in range(nq)]

    d_hidden = dot(r["gpA"][0], w[:, 0:128], 1, 1)
    for j in range(1, nx):
        d_hidden = d_hidden + dot(r["gpA"][j], w[:, j * 128:(j + 1) * 128], 1, 1)
    r["o_dh"][...] = d_hidden.astype(BF16)

    def along(axis, d):
        return (dev((z + d) % nz, y, c, x), (z + d) % nz) if axis == 0 else (dev(z, (y + d) % ny, c, x), (y + d) % ny)

    here = (z, y)
    orders = (z_order, y_order)
    counts = (nz, ny)
    w_copy.wait_recv()
    first_sems = [sems.take() for _ in range(nq)]
    for j in range(nq):
        both = own_dw[j] + r["rDW"][j].astype(F32)
        axis = j % 2
        size = 512 // counts[axis]
        for i in range(counts[axis]):
            r[f"dw{j}a"][i] = both[i * size:(i + 1) * size].astype(BF16)
        for d in orders[axis]:
            device, to = along(axis, d)
            rc(r[f"dw{j}a"].at[to], r[f"rd{j}a"].at[here[axis]], first_sems[j], device).start()
        leave(r[f"dw{j}a"].at[0:counts[axis] - 1], first_sems[j])
        r[f"rd{j}a"][here[axis]] = r[f"dw{j}a"][here[axis]]

    for at in range(nz - 1):
        part = r["rC2"].at[0:nz - 1 - at]
        when(z == at, rc(part, part, f_sem, partner).wait_recv)
    r["rC2"][z] = jnp.zeros((ch, 128), BF16)
    for i in range(nz):
        @pl.when(i < z)
        def _():
            r["rC2"][i] = jnp.zeros((ch, 128), BF16)
    from_z = r["rC2"][0].astype(F32)
    for i in range(1, nz):
        from_z = from_z + r["rC2"][i].astype(F32)
    for i in range(ny):
        value = from_z
        for later in range(i + 1, ny):
            value = value + r["rD"][later, (i ^ later).bit_length() - 1].astype(F32)
        r["R"][i] = value.astype(BF16)
    h_sem = sems.take()
    for d in y_order:
        to = (y + d) % ny
        rc(r["R"].at[to], r["adj"].at[rows(slot, ch)], h_sem, dev(z, to, c, x)).start()
    leave(chunks(ny - 1), h_sem)
    r["adj"][rows(slot, ch), :] = r["R"][y]

    second_sems = [sems.take() for _ in range(nq)]
    keep = ry // 2
    for j in range(nq):
        axis = j % 2
        arrive(r[f"rd{j}a"].at[0:counts[axis] - 1], first_sems[j])
        value = r[f"rd{j}a"][0].astype(F32)
        for i in range(1, counts[axis]):
            value = value + r[f"rd{j}a"][i].astype(F32)
        axis = 1 - axis
        count = counts[axis]
        for i in range(count):
            for t in range(2):
                r[f"dw{j}b"][2 * i + t] = value[i * ry + t * keep:i * ry + (t + 1) * keep]
        place = r[f"rd{j}b"].at[c * count + here[axis]]
        for d in [*orders[axis], 0]:
            spot = (here[axis] + d) % count
            for t in (1 - c, c)[:2 if d else 1]:
                device = dev(spot, y, t, x) if axis == 0 else dev(z, spot, t, x)
                rc(r[f"dw{j}b"].at[2 * spot + t], place, second_sems[j], device).start()
        leave(r[f"dw{j}b"].at[0:2 * count - 1], second_sems[j])
        r[f"rd{j}b"][c * count + here[axis]] = r[f"dw{j}b"][2 * here[axis] + c]

    arrive(chunks(ny - 1), h_sem)
    adj_share = rc(r["adj"].at[half], r["adj"].at[half], sems.take(), partner)
    adj_share.start()
    pending.append((None, adj_share))

    loaded("dst")
    adj_share.wait_recv()
    ga.wait_recv()
    first = (1 - c).astype(F32)

    def finish(p, carry):
        at = rows(p, 128)
        total = r["dst"][at, :] + r["adj"][at, :].astype(F32) + pG[0, at, :].astype(F32) * first
        wide = spread_pair(total.astype(BF16))
        dk2 = r["dk"][:, l128(p)] + dot(v[:, l256(p)], wide, 1, 1)
        r["o_dk"][:, l128(p)] = dk2.astype(BF16)
        dv2 = r["dv"][:, l256(p)] + mm(k[:, l128(p)], wide)
        r["o_dv"][:, l256(p)] = dv2.astype(BF16)
        return carry

    lax.fori_loop(0, 4, finish, 0)

    for j in range(nq):
        count = counts[1 - j % 2]
        arrive(r[f"rd{j}b"].at[0:2 * count - 1], second_sems[j])
        for t in range(2):
            value = r[f"rd{j}b"][t * count]
            for i in range(1, count):
                value = value + r[f"rd{j}b"][t * count + i]
            r["o_dw"][:, (t * nq + j) * 128:(t * nq + j + 1) * 128] = value

    assert sems.used == r["send"].shape[0]
    for cond, cp in pending:
        if cond is None:
            cp.wait_send()
        else:
            @pl.when(cond)
            def _():
                cp.wait_send()


def write_out(*refs):
    count = len(refs) // 2
    sem = refs[-1]
    copies = [pltpu.make_async_copy(refs[i], refs[count + i], sem.at[i]) for i in range(count)]
    for cp in copies:
        cp.start()
    for cp in copies:
        cp.wait()


def build(mesh, nz, ny):
    nx = mesh.shape["head"]
    ly, lz = ny.bit_length() - 1, nz.bit_length() - 1
    nl = 1 + ly + lz
    ch = T // ny
    nq = nx // 2
    rz = 512 // nz
    ry = rz // ny
    n_sem = 13 + 2 * (ly + lz) + 2 * nq
    select, member, level = segment_tables()
    levels_of = np.concatenate([level, np.full((128,), 8, np.int32)])[None]
    vm = pltpu.VMEM
    wide = nx * 128
    scratch = [
        vm((nx, T, 128), F32), vm((nx, T, 128), F32),
        vm((512, 128), BF16), vm((512, 128), F32), vm((512, 128), BF16), vm((T, 128), BF16),
        vm((ny, ch, 128), BF16), vm((max(ly, 1), max(ny // 2, 1), ch, 128), BF16), vm((ch, 128), BF16),
        vm((nz, ch, 128), BF16), vm((lz, ch, 128), BF16), vm((nl, 512, 128), BF16),
        vm((4, T, nl * 128), BF16), vm((4, T, nl * 128), BF16),
        vm((nl, 512, 128), BF16), vm((nl, 512, 128), F32), vm((nl, 512, 128), BF16), vm((nl - 1, T, 128), BF16),
        vm((ny, nl - 1, ch, 128), BF16), vm((lz, ch, 128), BF16), vm((nz, ch, 128), BF16),
        vm((ny, ch, 128), BF16), vm((512, 128), BF16),
        vm((T, 1024), F32), vm((T, 512), F32), vm((T, 512), F32), vm((T, 1024), F32),
        vm((T, 128), F32), vm((T, 128), F32), vm((T, 256), BF16),
        vm((nx, T, 128), BF16),
        vm((nq, 512, 128), BF16), vm((nq, 512, 128), BF16),
        vm((nz, rz, 128), BF16), vm((nz, rz, 128), BF16),
        vm((ny, 512 // ny, 128), BF16), vm((ny, 512 // ny, 128), BF16),
        vm((2 * ny, ry // 2, 128), F32), vm((2 * ny, ry // 2, 128), F32),
        vm((2 * nz, ry // 2, 128), F32), vm((2 * nz, ry // 2, 128), F32),
        vm((T, 512), BF16), vm((512, wide), BF16), vm((T, 512), BF16), vm((T, 512), BF16),
        vm((T, 1024), BF16), vm((T, 1024), BF16), vm((512, 128), F32),
        vm((T, 256), BF16), vm((T, 128), BF16), vm((1, 384), jnp.int32),
        vm((8, 384, 128), F32), vm((8, 384, 128), F32), vm((T, 512), BF16),
        pltpu.SemaphoreType.DMA((n_sem,)), pltpu.SemaphoreType.DMA((n_sem,)), pltpu.SemaphoreType.DMA((10,)),
    ]

    results = [
        jax.ShapeDtypeStruct((T, 1024), BF16),
        jax.ShapeDtypeStruct((T, 512), BF16),
        jax.ShapeDtypeStruct((T, 512), BF16),
        jax.ShapeDtypeStruct((T, 1024), BF16),
        jax.ShapeDtypeStruct((T, 512), BF16),
        jax.ShapeDtypeStruct((ry // 2, wide), F32),
    ]

    def step(hidden, w, q, k, v, g, d_state):
        operands = (
            hidden, w, q, k, v, g, d_state.reshape(512, DV),
            jnp.asarray(select, BF16), jnp.asarray(member, BF16), jnp.asarray(levels_of),
        )
        outs = pl.pallas_call(
            functools.partial(kernel, (nz, ny, nx, ly, lz)),
            out_shape=[pltpu.VMEM(a.shape, a.dtype) for a in results],
            in_specs=[pl.BlockSpec(memory_space=pltpu.HBM)] * 10,
            out_specs=[pl.BlockSpec(memory_space=pltpu.VMEM)] * 6,
            scratch_shapes=scratch,
            compiler_params=pltpu.CompilerParams(
                collective_id=0, has_side_effects=True, vmem_limit_bytes=36 * 1024 * 1024
            ),
        )(
            *(pltpu.with_memory_space_constraint(a, pltpu.HBM) for a in operands)
        )
        return pl.pallas_call(
            write_out,
            out_shape=results,
            in_specs=[pl.BlockSpec(memory_space=pltpu.VMEM)] * 6,
            out_specs=[pl.BlockSpec(memory_space=pltpu.HBM)] * 6,
            scratch_shapes=[pltpu.SemaphoreType.DMA((6,))],
            compiler_params=pltpu.CompilerParams(vmem_limit_bytes=8 * 1024 * 1024),
        )(*outs)

    both = P("seq", "head")
    return jax.shard_map(
        step,
        mesh=mesh,
        in_specs=(both, P("head", None), both, both, both, both, P("head", None, None)),
        out_specs=(both, both, both, both, both, P(("head", "seq"), None)),
        check_vma=False,
    )


def solution(mesh):
    return build(mesh, 8, 8)
```

time: 234 us -> 56.7 us (0.24)
  waiting for transfers between devices: 82.1 us -> 0 us
  starting transfers between devices: 70 us -> 0 us
  Pallas kernels: 0 us -> 55.9 us
  matrix products: 38.9 us -> 0 us
  other arithmetic: 19.9 us -> 0 us
  local copies, waits for them, and re-layouts: 13.9 us -> 0 us
  blocking collectives: 6.78 us -> 0 us
    ppermute x14 -> x0, waiting for transfers between devices: 80.1 us -> none  [partner_2(): return lax.ppermute(value, axis, pairs)]
    pallas_call x0 -> x2, Pallas kernels: none -> 55.9 us  [the longest x1 54.6 us: step(): pl.pallas_call(functools.partial(kernel, (nz, ny, nx, ly, lz)), out_shape...]
    ppermute x14 -> x0, starting transfers between devices: 50.1 us -> none  [partner_2(): return lax.ppermute(value, axis, pairs)]
    dot_general x19 -> x0, matrix products: 38.9 us -> none  [the longest x1 6.68 us: local_pass(): carried = jnp.einsum('thkd,khdv->thv', scaled, states, precision=PRECISE)]
    all_to_all x3 -> x0, starting transfers between devices: 19.9 us -> none  [the longest x1 8.25 us: copy_for_each(): return lax.all_to_all(copies, axis, split_axis=0, concat_axis=0, tiled=True)]
    add x15 -> x0, other arithmetic: 8.91 us -> none  [the longest x7 4.91 us: body(): pending = adjoint + jnp.where(is_upper, state_grads[bit], 0.0)]
    unnamed x69 -> x0, local copies, waits for them, and re-layouts: 7.88 us -> none
    all_to_all x1 -> x0, blocking collectives: 6.78 us -> none  [summed_on_arrival(): lax.all_to_all(pieces, axis, split_axis=0, concat_axis=0, tiled=True)]
  transfers between devices with their start and end apart: 17 -> 0, of which waited for: 12 -> 0; matrix products, arithmetic and copies ran while one was open for 24% -> 0% of each run, Pallas kernels for 0% -> 0%
where the time goes in v1:
time: 56.7 us; the launch traced here: 56.5 us
  Pallas kernels  55.9 us (99%)
  between operations  0.64 us (1%)
    pallas_call x1, Pallas kernels, step(): pl.pallas_call(functools.partial(kernel, (nz, ny, nx, ly, lz)), out_shape...  54.6 us
    pallas_call x1, Pallas kernels, step(): pl.pallas_call(write_out, out_shape=results, in_specs=[pl.BlockSpec(memor...  1.28 us

profile of v1, /device:TPU:1, one launch (start us, length us, event | category | flops | bytes accessed | tf_op | source)
XLA Modules:
  0.0 56.5 jit_solution(6201365506682447709)
XLA Ops:
  0.6 54.6 %shard_map.145 = (bf16[256,1024]{1,0:T(8,128)(2,1)S(1)}, bf16[256,512]{1,0:T(8,128)(2,1)S(1)}, bf16[256,512]{1,0:T(8,128)(2,1)S(1)}, bf16[256,1024]{1,0:T(8,128)...) custom-call(bf16[256,512]{1,0:T(8,128)(2,1)} %refs_0_.1, bf16[512,512]{1,0:T(8,128)(2,1)} %refs_1_.1, ...), custom_call_target="tpu_custom_call" | custom-call | tf_op jit(solution)/shard_map/pallas_call | solution.py:669
  55.3 1.3 %shard_map.146 = (bf16[256,1024]{1,0:T(8,128)(2,1)}, bf16[256,512]{1,0:T(8,128)(2,1)}, bf16[256,512]{1,0:T(8,128)(2,1)}, bf16[256,1024]{1,0:T(8,128)(2,1)}, bf16[256,512]{1,0:T(8,128)(2,1)}, /*index=5*/f32[4,512]{1,0:T(4,128)}) custom-call(bf16[256,1024]{1,0:T(8,128)(2,1)S(1)} %get-tuple-element.12.refs_0_, bf16[256,512]{1,0:T(8,128)(2,1)S(1)} %get-tuple-element.13.refs_1_, ...), custom_call_target="tpu_custom_call" | custom-call | tf_op jit(solution)/shard_map/pallas_call | solution.py:681

commit v2 on v1

--- a/solution.py
+++ b/solution.py
@@ -65,7 +65,7 @@
         "part", "rX", "kv", "kvf", "pk", "S", "rB", "tY", "TT", "rC", "UZ", "U", "sQ", "lw2", "G", "Gf", "pG", "GS",
         "rD", "GZ", "rC2", "R", "adj", "oacc", "dq", "dk", "dv", "gl", "sig", "lwb", "gpA", "dws", "rDW", "dw0a", "rd0a", "dw1a", "rd1a",
         "dw0b", "rd0b", "dw1b", "rd1b",  "hid", "w", "q", "k", "v", "g", "dst", "sel", "mem", "lev",
-        "scs", "gms", "hidp", "send", "recv", "load",
+        "scs", "gms", "hidp", "swap", "gpL", "gpH", "send", "recv", "load",
     )
     r = dict(zip(names, refs, strict=True))
     hid, w, q, k, v, g = (r[n] for n in ("hid", "w", "q", "k", "v", "g"))
@@ -178,6 +178,12 @@
     wanted = ((col // ry) % nz) * rz + (col // (nz * ry)) * ry + col % ry
     r["hidp"][...] = mm(hid[...], jnp.where(src == wanted, 1.0, 0.0).astype(BF16)).astype(BF16)
 
+    src = lax.broadcasted_iota(jnp.int32, (T, T), 0)
+    col = lax.broadcasted_iota(jnp.int32, (T, T), 1)
+    level = src % LEVELS
+    packed = (level // 8) * 128 + (src // 128) * 64 + ((src % 128) // LEVELS) * 8 + level % 8
+    r["swap"][...] = jnp.where(col == packed, 1.0, 0.0).astype(BF16)
+
     a_copy.wait_recv()
     half = rows(c, T)
     mine = r["kvf"][half, :] + r["pk"][half, :].astype(F32)
@@ -204,7 +210,7 @@
         q2 = q[:, l128(p)]
         k2 = k[:, l128(p)]
         member = r["mem"][...]
-        gl = r["gl"][...]
+        gl = carry
         for i in range(2):
             mask = low if i == 0 else jnp.logical_not(low)
             qh = jnp.where(mask, q2, jnp.zeros_like(q2))
@@ -222,11 +228,9 @@
             gl = gl + dot(near, table[:, :256], 1, 1)
             far = dot(prod[256:], jnp.concatenate([table[:, 256:], table[:, 256:]], 1), 1, 1)
             gl = gl + jnp.concatenate([jnp.zeros((128, 128), F32), far], 0)
-        r["gl"][...] = gl
-        return carry
-
-    r["gl"][...] = jnp.zeros((T, 128), F32)
-    lax.fori_loop(0, 4, scores, 0)
+        return gl
+
+    r["gl"][...] = lax.fori_loop(0, 4, scores, jnp.zeros((T, 128), F32), unroll=4)
 
     arrive(chunks(ny - 1), b_sem)
     sums = [r["rB"][i].astype(F32) for i in range(ny)]
@@ -298,7 +302,7 @@
             G[m, rows(p, 128), :] = state.astype(BF16)
         return carry
 
-    lax.fori_loop(0, 4, grad_states, 0)
+    lax.fori_loop(0, 4, grad_states, 0, unroll=4)
     ga = rc(G.at[0], pG.at[0], sems.take(), partner)
     ga.start()
     pending.append((None, ga))
@@ -345,8 +349,6 @@
         r["dk"][:, l128(p)] = dk2
         return carry
 
-    lax.fori_loop(0, 1, local_pair, 0)
-
     for at in range(1, nz):
         when(z == at, rc(r["rC"].at[0:at], r["rC"].at[0:at], c_sem, partner).wait_recv)
     for level in range(lz):
@@ -377,6 +379,8 @@
 
     share_y = shared(0, ly)
 
+    lax.fori_loop(0, 1, local_pair, 0)
+
     gb.wait_recv()
     for level in range(ly + lz):
         both = r["Gf"][1 + level, half, :] + pG[1 + level, half, :].astype(F32)
@@ -395,7 +399,7 @@
                 ).start()
             r["rD"][y, level] = r["GS"][level, rows(y, ch), :]
 
-    lax.fori_loop(1, 4, local_pair, 0)
+    lax.fori_loop(1, 4, local_pair, 0, unroll=3)
 
     def states_of(p, first, last):
         return jnp.concatenate([spread_pair(U[m, rows(p, 128), :]) for m in range(first, last)], 0)
@@ -409,7 +413,7 @@
         table = jnp.where(
             out_col == (2 * p + (out_row % 128) // DK) * LEVELS + BASE + first + out_row // 256, 1.0, 0.0
         ).astype(BF16)
-        r["gl"][...] += mm(jnp.concatenate(terms, 1), table)
+        return mm(jnp.concatenate(terms, 1), table)
 
     def add_states(p, back, wide, first, last):
         columns = slice(first * 128, last * 128)
@@ -423,15 +427,14 @@
     def near_levels(p, carry):
         wide = states_of(p, 0, 1 + ly)
         back = dot(g[:, l256(p)], wide, 1, 1)
-        add_levels(p, back, 0, 1 + ly)
+        carry = carry + add_levels(p, back, 0, 1 + ly)
         out, dq2 = add_states(p, back, wide, 0, 1 + ly)
         r["oacc"][:, l256(p)] = out
         r["dq"][:, l128(p)] = dq2
         return carry
 
     def far_levels(p, carry):
-        add_levels(p, dot(g[:, l256(p)], states_of(p, 1 + ly, nl), 1, 1), 1 + ly, nl)
-        return carry
+        return carry + add_levels(p, dot(g[:, l256(p)], states_of(p, 1 + ly, nl), 1, 1), 1 + ly, nl)
 
     def far_states(p, carry):
         wide = states_of(p, 1 + ly, nl)
@@ -440,20 +443,44 @@
         r["o_dq"][:, l128(p)] = dq2.astype(BF16)
         return carry
 
+    def send_levels(gl, part, place):
+        gp = (gl * r["sig"][...]).astype(BF16)
+        sides = jnp.concatenate([gp[:128], gp[128:]], 1)
+        place[x] = mm(sides, r["swap"][:, part * 128:(part + 1) * 128]).astype(BF16)
+        sem = sems.take()
+        for d in x_order:
+            to = (x + d) % nx
+            rc(place.at[x], place.at[x], sem, dev(z, y, c, to)).start()
+        leave(place.at[0:nx - 1], sem)
+        return sem
+
+    low_sem = send_levels(r["gl"][...], 0, r["gpL"])
+
     share_y.wait_recv()
-    lax.fori_loop(0, 4, near_levels, 0)
+    near = lax.fori_loop(0, 4, near_levels, r["gl"][...], unroll=4)
+    r["gl"][...] = near
     share_z = shared(ly, ly + lz)
     share_z.wait_recv()
-    lax.fori_loop(0, 4, far_levels, 0)
-    gp = (r["gl"][...] * r["sig"][...]).astype(BF16)
-    r["gpA"][x] = gp
-    g_sem = sems.take()
-    for d in x_order:
-        to = (x + d) % nx
-        rc(r["gpA"].at[x], r["gpA"].at[x], g_sem, dev(z, y, c, to)).start()
-    leave(r["gpA"].at[0:nx - 1], g_sem)
-
-    lax.fori_loop(0, 4, far_states, 0)
+    gl = lax.fori_loop(0, 4, far_levels, r["gl"][...], unroll=4)
+    high_sem = send_levels(gl, 1, r["gpH"])
+
+    lax.fori_loop(0, 4, far_states, 0, unroll=4)
+
+    arrive(r["gpL"].at[0:nx - 1], low_sem)
+    arrive(r["gpH"].at[0:nx - 1], high_sem)
+    for j in range(nx):
+        sides = jnp.concatenate([r["gpL"][j], r["gpH"][j]], 1)
+        sides = dot(sides, r["swap"][...], 1, 1).astype(BF16)
+        r["gpA"][j] = jnp.concatenate([sides[:, :128], sides[:, 128:]], 0)
+    def left(j):
+        return hid[...] if j % 2 == 0 else r["hidp"][...]
+
+    for j in range(nq):
+        r["dws"][j] = dot(left(j), r["gpA"][(1 - c) * nq + j], 0, 0).astype(BF16)
+    w_copy = rc(r["dws"], r["rDW"], sems.take(), partner)
+    w_copy.start()
+    pending.append((None, w_copy))
+    own_dw = [dot(left(j), r["gpA"][c * nq + j], 0, 0) for j in range(nq)]
 
     for level in range(ly + lz):
         if level >= ly:
@@ -483,17 +510,6 @@
     for at in range(1, nz):
         leave(r["rC2"].at[0:at], f_sem, z == at)
 
-    arrive(r["gpA"].at[0:nx - 1], g_sem)
-    def left(j):
-        return hid[...] if j % 2 == 0 else r["hidp"][...]
-
-    for j in range(nq):
-        r["dws"][j] = dot(left(j), r["gpA"][(1 - c) * nq + j], 0, 0).astype(BF16)
-    w_copy = rc(r["dws"], r["rDW"], sems.take(), partner)
-    w_copy.start()
-    pending.append((None, w_copy))
-    own_dw = [dot(left(j), r["gpA"][c * nq + j], 0, 0) for j in range(nq)]
-
     d_hidden = dot(r["gpA"][0], w[:, 0:128], 1, 1)
     for j in range(1, nx):
         d_hidden = d_hidden + dot(r["gpA"][j], w[:, j * 128:(j + 1) * 128], 1, 1)
@@ -584,7 +600,7 @@
         r["o_dv"][:, l256(p)] = dv2.astype(BF16)
         return carry
 
-    lax.fori_loop(0, 4, finish, 0)
+    lax.fori_loop(0, 4, finish, 0, unroll=4)
 
     for j in range(nq):
         count = counts[1 - j % 2]
@@ -623,7 +639,7 @@
     nq = nx // 2
     rz = 512 // nz
     ry = rz // ny
-    n_sem = 13 + 2 * (ly + lz) + 2 * nq
+    n_sem = 14 + 2 * (ly + lz) + 2 * nq
     select, member, level = segment_tables()
     levels_of = np.concatenate([level, np.full((128,), 8, np.int32)])[None]
     vm = pltpu.VMEM
@@ -649,6 +665,7 @@
         vm((T, 1024), BF16), vm((T, 1024), BF16), vm((512, 128), F32),
         vm((T, 256), BF16), vm((T, 128), BF16), vm((1, 384), jnp.int32),
         vm((8, 384, 128), F32), vm((8, 384, 128), F32), vm((T, 512), BF16),
+        vm((T, T), BF16), vm((nx, 128, 128), BF16), vm((nx, 128, 128), BF16),
         pltpu.SemaphoreType.DMA((n_sem,)), pltpu.SemaphoreType.DMA((n_sem,)), pltpu.SemaphoreType.DMA((10,)),
     ]
 

time: 56.7 us -> 54.7 us (0.965)
  Pallas kernels: 55.9 us -> 53.8 us
    pallas_call x1, Pallas kernels: 54.6 us -> 52.5 us  [step(): pl.pallas_call(functools.partial(kernel, (nz, ny, nx, ly, lz)), out_shape...]
where the time goes in v2:
time: 54.7 us; the launch traced here: 54.6 us
  Pallas kernels  53.8 us (98%)
  between operations  0.8 us (1%)
    pallas_call x1, Pallas kernels, step(): pl.pallas_call(functools.partial(kernel, (nz, ny, nx, ly, lz)), out_shape...  52.5 us
    pallas_call x1, Pallas kernels, step(): pl.pallas_call(write_out, out_shape=results, in_specs=[pl.BlockSpec(memor...  1.28 us

profile of v2, /device:TPU:1, one launch (start us, length us, event | category | flops | bytes accessed | tf_op | source)
XLA Modules:
  0.0 54.6 jit_solution(780058626917711993)
XLA Ops:
  0.6 52.5 %shard_map.145 = (bf16[256,1024]{1,0:T(8,128)(2,1)S(1)}, bf16[256,512]{1,0:T(8,128)(2,1)S(1)}, bf16[256,512]{1,0:T(8,128)(2,1)S(1)}, bf16[256,1024]{1,0:T(8,128)...) custom-call(bf16[256,512]{1,0:T(8,128)(2,1)} %refs_0_.1, bf16[512,512]{1,0:T(8,128)(2,1)} %refs_1_.1, ...), custom_call_target="tpu_custom_call" | custom-call | tf_op jit(solution)/shard_map/pallas_call | solution.py:686
  53.2 1.3 %shard_map.146 = (bf16[256,1024]{1,0:T(8,128)(2,1)}, bf16[256,512]{1,0:T(8,128)(2,1)}, bf16[256,512]{1,0:T(8,128)(2,1)}, bf16[256,1024]{1,0:T(8,128)(2,1)}, bf16[256,512]{1,0:T(8,128)(2,1)}, /*index=5*/f32[4,512]{1,0:T(4,128)}) custom-call(bf16[256,1024]{1,0:T(8,128)(2,1)S(1)} %get-tuple-element.12.refs_0_, bf16[256,512]{1,0:T(8,128)(2,1)S(1)} %get-tuple-element.13.refs_1_, ...), custom_call_target="tpu_custom_call" | custom-call | tf_op jit(solution)/shard_map/pallas_call | solution.py:698

commit v3 on v2

--- a/solution.py
+++ b/solution.py
@@ -460,8 +460,12 @@
     near = lax.fori_loop(0, 4, near_levels, r["gl"][...], unroll=4)
     r["gl"][...] = near
     share_z = shared(ly, ly + lz)
+    gl = r["gl"][...]
+    for i in range(2):
+        gl = far_levels(2 * c + i, gl)
     share_z.wait_recv()
-    gl = lax.fori_loop(0, 4, far_levels, r["gl"][...], unroll=4)
+    for i in range(2):
+        gl = far_levels(2 * (1 - c) + i, gl)
     high_sem = send_levels(gl, 1, r["gpH"])
 
     lax.fori_loop(0, 4, far_states, 0, unroll=4)
@@ -586,7 +590,6 @@
     pending.append((None, adj_share))
 
     loaded("dst")
-    adj_share.wait_recv()
     ga.wait_recv()
     first = (1 - c).astype(F32)
 
@@ -600,7 +603,11 @@
         r["o_dv"][:, l256(p)] = dv2.astype(BF16)
         return carry
 
-    lax.fori_loop(0, 4, finish, 0, unroll=4)
+    for i in range(2):
+        finish(2 * c + i, 0)
+    adj_share.wait_recv()
+    for i in range(2):
+        finish(2 * (1 - c) + i, 0)
 
     for j in range(nq):
         count = counts[1 - j % 2]

time: 54.7 us -> 55.4 us (1.013)
  Pallas kernels: 53.8 us -> 54.4 us
    pallas_call x1, Pallas kernels: 52.5 us -> 53.2 us  [step(): pl.pallas_call(functools.partial(kernel, (nz, ny, nx, ly, lz)), out_shape...]
where the time goes in v3:
time: 55.4 us; the launch traced here: 55.2 us
  Pallas kernels  54.4 us (98%)
  between operations  0.8 us (1%)
    pallas_call x1, Pallas kernels, step(): pl.pallas_call(functools.partial(kernel, (nz, ny, nx, ly, lz)), out_shape...  53.2 us
    pallas_call x1, Pallas kernels, step(): pl.pallas_call(write_out, out_shape=results, in_specs=[pl.BlockSpec(memor...  1.28 us

profile of v3, /device:TPU:1, one launch (start us, length us, event | category | flops | bytes accessed | tf_op | source)
XLA Modules:
  0.0 55.2 jit_solution(5745351380392470632)
XLA Ops:
  0.6 53.2 %shard_map.145 = (bf16[256,1024]{1,0:T(8,128)(2,1)S(1)}, bf16[256,512]{1,0:T(8,128)(2,1)S(1)}, bf16[256,512]{1,0:T(8,128)(2,1)S(1)}, bf16[256,1024]{1,0:T(8,128)...) custom-call(bf16[256,512]{1,0:T(8,128)(2,1)} %refs_0_.1, bf16[512,512]{1,0:T(8,128)(2,1)} %refs_1_.1, ...), custom_call_target="tpu_custom_call" | custom-call | tf_op jit(solution)/shard_map/pallas_call | solution.py:693
  53.8 1.3 %shard_map.146 = (bf16[256,1024]{1,0:T(8,128)(2,1)}, bf16[256,512]{1,0:T(8,128)(2,1)}, bf16[256,512]{1,0:T(8,128)(2,1)}, bf16[256,1024]{1,0:T(8,128)(2,1)}, bf16[256,512]{1,0:T(8,128)(2,1)}, /*index=5*/f32[4,512]{1,0:T(4,128)}) custom-call(bf16[256,1024]{1,0:T(8,128)(2,1)S(1)} %get-tuple-element.12.refs_0_, bf16[256,512]{1,0:T(8,128)(2,1)S(1)} %get-tuple-element.13.refs_1_, ...), custom_call_target="tpu_custom_call" | custom-call | tf_op jit(solution)/shard_map/pallas_call | solution.py:705
